TPU v7x, 32 devices: a whole 2x2x4 slice. The times are simulated.
32 devices in a mesh: seq: 8 (over z, x), group: 4 (over y, core).
Axes of the slice: x: 2, y: 2, z: 4, core: 2. Of those that a mesh axis runs over, the one named last changes fastest.
Arguments:
- new_queries: bfloat16 [8, 8, 8, 128], P('seq', 'group'), may hold values from -6 to 6
- stored_keys: bfloat16 [8, 8, 4096, 128], P(None, 'group', 'seq'), may hold values from -6 to 6
- stored_values: bfloat16 [8, 8, 4096, 128], P(None, 'group', 'seq'), may hold values from -6 to 6
- used_length: int32 [8], replicated, may hold values from 2048 to 4096
- out_weight: bfloat16 [8, 8, 128, 5120], P('group'), may hold values from -0.0625 to 0.0625
Outputs:
- token_out: bfloat16 [8, 5120], P('seq', 'group')
All inputs are finite; a program needn't handle non-finite values.
Results may differ from a plain program's by a relative error of at most 0.0025.
Values may be sent and summed in bfloat16 or wider, within the bound.
A program may use at most 128 MiB of HBM per device.

v0:
```python
import jax
import jax.numpy as jnp
from jax import lax
from jax.sharding import PartitionSpec as P

HEAD_SIZE = 128


def per_device(new_queries, stored_keys, stored_values, used_length, out_weight):
    all_queries = lax.all_gather(new_queries, "seq", axis=0, tiled=True)
    logit = jnp.einsum(
        "bkgd,bktd->bkgt", all_queries, stored_keys, preferred_element_type=jnp.float32
    ) * HEAD_SIZE ** (-0.5)
    positions = lax.axis_index("seq") * stored_keys.shape[2] + jnp.arange(stored_keys.shape[2])
    filled = positions[None, :] < used_length[:, None]
    logit = jnp.where(filled[:, None, None, :], logit, -1e30)
    top = jnp.max(logit, axis=-1)
    part = jnp.where(filled[:, None, None, :], jnp.exp(logit - top[..., None]), 0.0)
    weight_sum = jnp.sum(part, axis=-1)
    read_sum = jnp.einsum(
        "bkgt,bktd->bkgd", part, stored_values.astype(jnp.float32), precision=lax.Precision.HIGHEST
    )
    tops, sums, parts = (
        lax.all_to_all(top[None], "seq", split_axis=1, concat_axis=0, tiled=True),
        lax.all_to_all(weight_sum[None], "seq", split_axis=1, concat_axis=0, tiled=True),
        lax.all_to_all(read_sum[None], "seq", split_axis=1, concat_axis=0, tiled=True),
    )
    best = jnp.max(tops, axis=0)
    scale = jnp.exp(tops - best)
    weight_own = jnp.sum(sums * scale, axis=0)
    read_own = jnp.sum(parts * scale[..., None], axis=0)
    read = (read_own / weight_own[..., None]).astype(jnp.bfloat16)
    term = jnp.einsum("bkgd,kgdm->bm", read, out_weight, preferred_element_type=jnp.float32)
    token_out = lax.psum_scatter(term, "group", scatter_dimension=1, tiled=True).astype(
        jnp.bfloat16
    )
    return token_out


def solution(mesh):
    in_specs = (
        P("seq", "group", None, None),
        P(None, "group", "seq", None),
        P(None, "group", "seq", None),
        P(),
        P("group", None, None, None),
    )
    out_specs = P("seq", "group")
    return jax.shard_map(
        per_device, mesh=mesh, in_specs=in_specs, out_specs=out_specs, check_vma=False
    )
```

profile of v0, /device:TPU:0, one launch (start us, length us, event | category | flops | bytes accessed | tf_op | source)
XLA Modules:
  0.0 127.6 jit_solution(323941841293693378)
XLA Ops:
  6.5 0.0 copy-start
  6.5 32.5 %all_gather.3 = bf16[8,2,8,128]{3,2,1,0:T(8,128)(2,1)S(1)} all-gather(bf16[1,2,8,128]{3,2,1,0:T(8,128)(2,1)} %param.5), channel_id=1, replica_groups=mesh['seq'=8,'group'=4] {'seq'}, dimensions={0}, use_global_device_ids=true | all-gather | bytes 36864 | tf_op jit(solution)/shard_map/all_gather | solution.py:10
  39.1 0.7 broadcast_compare_fusion
  39.8 0.0 copy-done
  39.8 1.3 %fusion.18 = (f32[8,2,8]{2,1,0:T(2,128)}, f32[8,2,8,512]{3,2,1,0:T(8,128)S(1)}) fusion(bf16[8,2,8,128]{3,2,1,0:T(8,128)(2,1)S(1)} %all_gather.3, bf16[8,2,512,128]{3,2,1,0:T(8,128)(2,1)S(1)} %copy-done, pred[8,512]{1,0:T(8,128)(4,1)S(1)} %broadcast_compare_fusion), kind=kOutput, calls=%fused_computation.25 | convolution fusion | flops 16973696 | bytes 2396672 | tf_op jit(solution)/shard_map/bkgd,bktd->bkgt/dot_general | solution.py:11
  41.2 5.5 %all-to-all-start.1 = ((f32[1,8,2,8]{3,2,0,1:T(2,128)}), f32[1,8,2,8]{3,2,0,1:T(2,128)S(1)}, u32[]{:S(2)}, u32[]{:S(2)}) async-start(f32[1,8,2,8]{3,2,0,1:T(2,128)} %bitcast.15), calls=%async_computation.1 | async-start | bytes 16384 | tf_op jit(solution)/shard_map/all_to_all | solution.py:24
  46.6 1.5 %fusion.6 = f32[8,2,8]{2,1,0:T(2,128)} fusion(f32[8,2,8,512]{3,2,1,0:T(8,128)S(1)} %get-tuple-element.6, f32[8,2,8]{2,1,0:T(2,128)} %get-tuple-element.5, pred[8,512]{1,0:T(8,128)(4,1)S(1)} %broadcast_compare_fusion), kind=kLoop, calls=%fused_computation.7 | loop fusion | flops 196480 | bytes 267264 | tf_op jit(solution)/shard_map/reduce_sum | solution.py:19
  48.1 5.0 %all-to-all-done.1 = f32[1,8,2,8]{3,2,0,1:T(2,128)S(1)} async-done(((f32[1,8,2,8]{3,2,0,1:T(2,128)}), f32[1,8,2,8]{3,2,0,1:T(2,128)S(1)}, u32[]{:S(2)}, u32[]{:S(2)}) %all-to-all-start.1) | async-done | bytes 544 | tf_op jit(solution)/shard_map/all_to_all | solution.py:24
  53.2 3.3 %all-to-all-start.2 = ((f32[1,8,2,8]{3,2,0,1:T(2,128)}), f32[1,8,2,8]{3,2,0,1:T(2,128)S(1)}, u32[]{:S(2)}, u32[]{:S(2)}) async-start(f32[1,8,2,8]{3,2,0,1:T(2,128)} %bitcast.16), calls=%async_computation.2 | async-start | bytes 16384 | tf_op jit(solution)/shard_map/all_to_all | solution.py:25
  56.5 3.2 %convolution_bitcast_fusion = f32[1,8,2,8,128]{4,3,2,0,1:T(8,128)} fusion(bf16[8,2,512,128]{3,2,1,0:T(8,128)(2,1)} %param.7, f32[8,2,8,512]{3,2,1,0:T(8,128)S(1)} %get-tuple-element.6, f32[8,2,8]{2,1,0:T(2,128)} %get-tuple-element.5, pred[8,512]{1,0:T(8,128)(4,1)S(1)} %broadcast_compare_fusion), kind=kOutput, calls=%fused_computation.5 | convolution fusion | flops 100794368 | bytes 2429440 | tf_op jit(solution)/shard_map/bkgt,bktd->bkgd/dot_general | solution.py:20
  59.7 3.3 %all-to-all-done.2 = f32[1,8,2,8]{3,2,0,1:T(2,128)S(1)} async-done(((f32[1,8,2,8]{3,2,0,1:T(2,128)}), f32[1,8,2,8]{3,2,0,1:T(2,128)S(1)}, u32[]{:S(2)}, u32[]{:S(2)}) %all-to-all-start.2) | async-done | bytes 544 | tf_op jit(solution)/shard_map/all_to_all | solution.py:25
  63.0 3.3 %all-to-all-start = ((f32[1,8,2,8,128]{4,3,2,0,1:T(8,128)}), f32[1,8,2,8,128]{4,3,2,0,1:T(8,128)S(1)}, u32[]{:S(2)}, u32[]{:S(2)}) async-start(f32[1,8,2,8,128]{4,3,2,0,1:T(8,128)} %convolution_bitcast_fusion), calls=%async_computation | async-start | bytes 131072 | tf_op jit(solution)/shard_map/all_to_all | solution.py:26
  66.4 0.0 reduce-scatter.4.cloned.1.call-start
  66.5 6.7 %all-to-all-done = f32[1,8,2,8,128]{4,3,2,0,1:T(8,128)S(1)} async-done(((f32[1,8,2,8,128]{4,3,2,0,1:T(8,128)}), f32[1,8,2,8,128]{4,3,2,0,1:T(8,128)S(1)}, u32[]{:S(2)}, u32[]{:S(2)}) %all-to-all-start) | async-done | bytes 65568 | tf_op jit(solution)/shard_map/all_to_all | solution.py:26
  73.2 0.1 fusion.10
  73.3 0.1 fusion.16
  73.4 13.4 %fusion.2 = f32[5120,1]{1,0:T(8,128)} fusion(bf16[2,8,128,5120]{3,2,1,0:T(8,128)(2,1)} %param.9, bf16[2,8,128,1]{2,1,0,3:T(8,128)(2,1)S(1)} %fusion.16), kind=kOutput, calls=%fused_computation.2 | convolution fusion | flops 20971520 | bytes 20996096 | tf_op jit(solution)/shard_map/bkgd,kgdm->bm/dot_general | solution.py:33
  86.8 0.0 reduce-scatter.4.cloned.1.call-update
  86.8 32.0 %reduce-scatter.4.cloned.1.call-done = f32[1280,1]{1,0:T(8,128)} async-done(((f32[5120,1]{1,0:T(8,128)}), f32[1280,1]{1,0:T(8,128)}) %reduce-scatter.4.cloned.1.call-update) | async-done | bytes 5136
  118.9 1.9 %copy.25 = bf16[1,1280]{1,0:T(2,128)(2,1)} copy(f32[1,1280]{0,1:T(8,128)} %bitcast.43) | data formatting | bytes 7680
  (5 shorter events, 0.1 us)
Async XLA Ops:
  6.5 33.3 %copy-start = (bf16[8,2,512,128]{3,2,1,0:T(8,128)(2,1)S(1)}, bf16[8,2,512,128]{3,2,1,0:T(8,128)(2,1)}, u32[]{:S(2)}) copy-start(bf16[8,2,512,128]{3,2,1,0:T(8,128)(2,1)} %param.6) | copy-start | bytes 6291460
  41.2 12.0 %all-to-all-start.1 = ((f32[1,8,2,8]{3,2,0,1:T(2,128)}), f32[1,8,2,8]{3,2,0,1:T(2,128)S(1)}, u32[]{:S(2)}, u32[]{:S(2)}) async-start(f32[1,8,2,8]{3,2,0,1:T(2,128)} %bitcast.15), calls=%async_computation.1 | async-start | bytes 16384 | tf_op jit(solution)/shard_map/all_to_all | solution.py:24
  53.2 9.8 %all-to-all-start.2 = ((f32[1,8,2,8]{3,2,0,1:T(2,128)}), f32[1,8,2,8]{3,2,0,1:T(2,128)S(1)}, u32[]{:S(2)}, u32[]{:S(2)}) async-start(f32[1,8,2,8]{3,2,0,1:T(2,128)} %bitcast.16), calls=%async_computation.2 | async-start | bytes 16384 | tf_op jit(solution)/shard_map/all_to_all | solution.py:25
  63.0 10.2 %all-to-all-start = ((f32[1,8,2,8,128]{4,3,2,0,1:T(8,128)}), f32[1,8,2,8,128]{4,3,2,0,1:T(8,128)S(1)}, u32[]{:S(2)}, u32[]{:S(2)}) async-start(f32[1,8,2,8,128]{4,3,2,0,1:T(8,128)} %convolution_bitcast_fusion), calls=%async_computation | async-start | bytes 131072 | tf_op jit(solution)/shard_map/all_to_all | solution.py:26
  66.4 52.5 %reduce-scatter.4.cloned.1.call-start = ((), (), s32[]{:S(2)}) async-start(), calls=%async_computation.4 | async-start | bytes 3276800
Sparse Core Ops, SparseCore 0:
  86.9 31.8 reduce-scatter.3
where the time goes:
time: 128 us
  waiting for transfers between devices  47.1 us (37%)
  blocking collectives  32.5 us (25%)
  matrix products  18 us (14%)
  between operations  13.4 us (10%)
  starting transfers between devices  12.1 us (9%)
  other arithmetic  2.43 us (2%)
  local copies, waits for them, and re-layouts  1.92 us (2%)
    all_gather x1, blocking collectives, per_device(): all_queries = lax.all_gather(new_queries, 'seq', axis=0, tiled=True)  32.5 us
    unnamed x2, waiting for transfers between devices  32.1 us
    dot_general x1, matrix products, per_device(): jnp.einsum('bkgd,kgdm->bm', read, out_weight, preferred_element_type=jnp....  13.4 us
    all_to_all x1, waiting for transfers between devices, per_device(): lax.all_to_all(read_sum[None], 'seq', split_axis=1, concat_axis=0, tiled=...  6.74 us
    all_to_all x1, starting transfers between devices, per_device(): lax.all_to_all(top[None], 'seq', split_axis=1, concat_axis=0, tiled=True)  5.46 us
    all_to_all x1, waiting for transfers between devices, per_device(): lax.all_to_all(top[None], 'seq', split_axis=1, concat_axis=0, tiled=True)  5.04 us
    all_to_all x1, starting transfers between devices, per_device(): lax.all_to_all(read_sum[None], 'seq', split_axis=1, concat_axis=0, tiled=...  3.35 us
    all_to_all x1, waiting for transfers between devices, per_device(): lax.all_to_all(weight_sum[None], 'seq', split_axis=1, concat_axis=0, tile...  3.3 us
  transfers between devices with their start and end apart: 4, of which 4 were waited for; matrix products, arithmetic and copies ran while one was open for 4% of the time, Pallas kernels for 0%

commit v1 on v0

v1 whole, which is shorter than its diff:
```python
import functools

import jax
import jax.numpy as jnp
from jax import lax
from jax.experimental import pallas as pl
from jax.experimental.pallas import tpu as pltpu
from jax.sharding import PartitionSpec as P

MESH = pl.DeviceIdType.MESH
CLUSTER = 2


def kernel(
    n, ng, cluster, scale,
    q_hbm, k_hbm, v_hbm, used, w_hbm, out_ref,
    q_own, q_all, k_v, v_v, w_v, acc_buf, parts, stat_buf, stats, coef, lhs, term, landed,
    local_sem, k_sem, v_sem, w_sem, q_send, q_recv, s_send, s_recv, a_send, a_recv, t_send, t_recv,
):
    me, mg = lax.axis_index("seq"), lax.axis_index("group")
    batch, heads, stretch, size = k_v.shape
    rows = q_own.shape[0]
    per_head = rows // heads
    rf = rows // cluster
    base, f = (me // cluster) * cluster, lax.rem(me, cluster)
    width = out_ref.shape[1]
    depth = rf * size

    q_load = pltpu.make_async_copy(q_hbm, q_own, local_sem.at[0])
    q_load.start()

    barrier = pltpu.get_barrier_semaphore()
    peers = 0
    for j in range(1, n):
        pl.semaphore_signal(
            barrier, inc=1, device_id={"seq": lax.rem(me + j, n), "group": mg}, device_id_type=MESH
        )
        peers += 1
    for dj in range(cluster):
        for dg in range(1, ng):
            pl.semaphore_signal(
                barrier,
                inc=1,
                device_id={"seq": base + lax.rem(f + dj, cluster), "group": lax.rem(mg + dg, ng)},
                device_id_type=MESH,
            )
            peers += 1

    k_loads = [pltpu.make_async_copy(k_hbm.at[b], k_v.at[b], k_sem.at[b]) for b in range(batch)]
    v_loads = [pltpu.make_async_copy(v_hbm.at[b], v_v.at[b], v_sem.at[b]) for b in range(batch)]
    w_row = pl.multiple_of(f * depth, depth)
    w_loads = [
        pltpu.make_async_copy(
            w_hbm.at[pl.ds(w_row, depth), pl.ds(g * width, width)], w_v.at[g], w_sem.at[g]
        )
        for g in range(ng)
    ]
    for load in k_loads + v_loads + w_loads:
        load.start()

    q_load.wait()
    q_keep = pltpu.make_async_copy(q_own, q_all.at[me], local_sem.at[1])
    q_keep.start()
    pl.semaphore_wait(barrier, peers)

    def to_seq(src, dst, send, recv, j):
        return pltpu.make_async_remote_copy(
            src_ref=src, dst_ref=dst, send_sem=send.at[j], recv_sem=recv.at[j],
            device_id={"seq": lax.rem(me + j, n), "group": mg}, device_id_type=MESH,
        )

    q_out = [to_seq(q_own, q_all.at[me], q_send, q_recv, j) for j in range(1, n)]
    for copy in q_out:
        copy.start()
    lhs[...] = jnp.zeros_like(lhs)
    for load in k_loads:
        load.wait()
    q_keep.wait()
    for copy in q_out:
        copy.wait_recv()

    place = me * stretch + lax.broadcasted_iota(jnp.int32, (rows, stretch), 1)
    shares, tops, sums = [], [], []
    for b in range(batch):
        q = q_all[b]
        split_q = jnp.concatenate(
            [
                jnp.where(lax.broadcasted_iota(jnp.int32, (rows, size), 0) // per_head == h, q, jnp.zeros_like(q))
                for h in range(heads)
            ],
            axis=1,
        )
        keys = jnp.concatenate([k_v[b, h] for h in range(heads)], axis=1)
        logit = lax.dot_general(
            split_q, keys, (((1,), (1,)), ((), ())), preferred_element_type=jnp.float32
        ) * scale
        filled = place < used[b]
        logit = jnp.where(filled, logit, -1e30)
        top = jnp.max(logit, axis=1, keepdims=True)
        part = jnp.where(filled, jnp.exp(logit - top), 0.0)
        tops.append(top)
        sums.append(jnp.sum(part, axis=1, keepdims=True))
        shares.append(part)

    all_tops = jnp.concatenate(tops, axis=0)
    all_sums = jnp.concatenate(sums, axis=0)
    lane = lax.broadcasted_iota(jnp.int32, (batch * rows, 128), 1)
    stat_buf[...] = jnp.where(lane == 0, all_tops, all_sums).T[:2]
    s_out = [to_seq(stat_buf, stats.at[me], s_send, s_recv, j) for j in range(1, n)]
    for copy in s_out:
        copy.start()
    s_keep = pltpu.make_async_copy(stat_buf, stats.at[me], local_sem.at[2])
    s_keep.start()

    for load in v_loads:
        load.wait()
    for b in range(batch):
        part = shares[b]
        high = part.astype(jnp.bfloat16)
        low = (part - high.astype(jnp.float32)).astype(jnp.bfloat16)
        values = jnp.concatenate([v_v[b, h] for h in range(heads)], axis=1)
        both = jnp.dot(
            jnp.concatenate([high, low], axis=0), values, preferred_element_type=jnp.float32
        )
        both = both[:rows] + both[rows:]
        read = jnp.concatenate(
            [
                both[h * per_head : (h + 1) * per_head, h * size : (h + 1) * size]
                for h in range(heads)
            ],
            axis=0,
        )
        c, at = b // cluster, b % cluster
        for piece in range(cluster):
            acc_buf[c * cluster + piece, at * rf : (at + 1) * rf] = read[piece * rf : (piece + 1) * rf]

    a_out = [
        to_seq(acc_buf.at[lax.rem(me + j, n)], parts.at[me], a_send, a_recv, j) for j in range(1, n)
    ]
    for copy in a_out:
        copy.start()
    a_keep = pltpu.make_async_copy(acc_buf.at[me], parts.at[me], local_sem.at[3])
    a_keep.start()

    s_keep.wait()
    for copy in s_out:
        copy.wait_recv()
    m_all, s_all = stats[:, 0, :], stats[:, 1, :]
    weight = jnp.exp(m_all - jnp.max(m_all, axis=0, keepdims=True))
    weight = weight / jnp.sum(weight * s_all, axis=0, keepdims=True)
    weight = jnp.concatenate([weight, jnp.zeros((128 - n, batch * rows), jnp.float32)], axis=0)
    coef[...] = weight.T
    own = jnp.concatenate(
        [coef[pl.ds(pl.multiple_of((base + at) * rows + f * rf, rf), rf)] for at in range(cluster)],
        axis=0,
    )
    a_keep.wait()
    for copy in a_out:
        copy.wait_recv()
    read = own[:, 0:1] * parts[0]
    for src in range(1, n):
        read += own[:, src : src + 1] * parts[src]
    for at in range(cluster):
        for r in range(rf):
            lhs[at : at + 1, r * size : (r + 1) * size] = read[at * rf + r : at * rf + r + 1]
    token = lhs[...].astype(jnp.bfloat16)

    for load in w_loads:
        load.wait()
    t_out = []
    for dg in [*range(1, ng), 0]:
        g = lax.rem(mg + dg, ng)
        out = jnp.dot(token, w_v[g], preferred_element_type=jnp.float32)
        for at in range(cluster):
            term[g, at] = out[at : at + 1]
        for dj in range(cluster):
            at = lax.rem(f + dj, cluster)
            slot = f * ng + mg
            if dg == 0 and dj == 0:
                t_keep = pltpu.make_async_copy(term.at[g, at], landed.at[slot], local_sem.at[4])
                t_keep.start()
                continue
            copy = pltpu.make_async_remote_copy(
                src_ref=term.at[g, at], dst_ref=landed.at[slot],
                send_sem=t_send.at[dj * ng + dg], recv_sem=t_recv.at[dj * ng + dg],
                device_id={"seq": base + at, "group": g}, device_id_type=MESH,
            )
            copy.start()
            t_out.append(copy)
    t_keep.wait()
    for copy in t_out:
        copy.wait_recv()
    total = landed[0]
    for slot in range(1, cluster * ng):
        total += landed[slot]
    out_ref[...] = total.astype(out_ref.dtype)
    for copy in q_out + s_out + a_out + t_out:
        copy.wait_send()


def solution(mesh):
    n, ng = mesh.shape["seq"], mesh.shape["group"]

    def per_device(new_queries, stored_keys, stored_values, used_length, out_weight):
        batch, heads, stretch, size = stored_keys.shape
        group = new_queries.shape[2]
        rows = heads * group
        model = out_weight.shape[-1]
        cluster, width = CLUSTER, model // ng
        rf = rows // cluster
        dma = pltpu.SemaphoreType.DMA
        anywhere = pl.BlockSpec(memory_space=pl.ANY)
        f32, bf16 = jnp.float32, jnp.bfloat16
        return pl.pallas_call(
            functools.partial(kernel, n, ng, cluster, size ** (-0.5)),
            out_shape=jax.ShapeDtypeStruct((1, width), bf16),
            in_specs=[anywhere, anywhere, anywhere, pl.BlockSpec(memory_space=pltpu.SMEM), anywhere],
            out_specs=pl.BlockSpec(memory_space=pltpu.VMEM),
            scratch_shapes=[
                pltpu.VMEM((rows, size), bf16),
                pltpu.VMEM((n, rows, size), bf16),
                pltpu.VMEM(stored_keys.shape, bf16),
                pltpu.VMEM(stored_values.shape, bf16),
                pltpu.VMEM((ng, rf * size, width), bf16),
                pltpu.VMEM((n, rows, size), f32),
                pltpu.VMEM((n, rows, size), f32),
                pltpu.VMEM((2, batch * rows), f32),
                pltpu.VMEM((n, 2, batch * rows), f32),
                pltpu.VMEM((batch * rows, 128), f32),
                pltpu.VMEM((8, rf * size), f32),
                pltpu.VMEM((ng, cluster, 1, width), f32),
                pltpu.VMEM((cluster * ng, 1, width), f32),
                dma((5,)), dma((batch,)), dma((batch,)), dma((ng,)),
                dma((n,)), dma((n,)), dma((n,)), dma((n,)), dma((n,)), dma((n,)),
                dma((cluster * ng,)), dma((cluster * ng,)),
            ],
            compiler_params=pltpu.CompilerParams(collective_id=0, has_side_effects=True),
        )(
            new_queries.reshape(rows, size),
            stored_keys,
            stored_values,
            used_length,
            out_weight.reshape(rows * size, model),
        )

    return jax.shard_map(
        per_device,
        mesh=mesh,
        in_specs=(
            P("seq", "group", None, None),
            P(None, "group", "seq", None),
            P(None, "group", "seq", None),
            P(),
            P("group", None, None, None),
        ),
        out_specs=P("seq", "group"),
        check_vma=False,
    )
```

time: 128 us -> 23.8 us (0.19)
  waiting for transfers between devices: 47.1 us -> 0 us
  blocking collectives: 32.5 us -> 0 us
  Pallas kernels: 0 us -> 22.3 us
  matrix products: 18 us -> 0 us
  between operations: 13.4 us -> 0.01 us
  starting transfers between devices: 12.1 us -> 0 us
  other arithmetic: 2.43 us -> 0 us
    all_gather x1 -> x0, blocking collectives: 32.5 us -> none  [per_device(): all_queries = lax.all_gather(new_queries, 'seq', axis=0, tiled=True)]
    unnamed x2 -> x0, waiting for transfers between devices: 32.1 us -> none
    pallas_call x0 -> x1, Pallas kernels: none -> 22.3 us  [per_device(): pl.pallas_call(functools.partial(kernel, n, ng, cluster, size ** (-0.5)),...]
    dot_general x3 -> x0, matrix products: 18 us -> none  [the longest x1 13.4 us: per_device(): jnp.einsum('bkgd,kgdm->bm', read, out_weight, preferred_element_type=jnp....]
    all_to_all x3 -> x0, waiting for transfers between devices: 15.1 us -> none  [the longest x1 6.74 us: per_device(): lax.all_to_all(read_sum[None], 'seq', split_axis=1, concat_axis=0, tiled=...]
    all_to_all x3 -> x0, starting transfers between devices: 12.1 us -> none  [the longest x1 5.46 us: per_device(): lax.all_to_all(top[None], 'seq', split_axis=1, concat_axis=0, tiled=True)]
    reduce_sum x3 -> x0, other arithmetic: 1.59 us -> none  [the longest x1 1.49 us: per_device(): weight_sum = jnp.sum(part, axis=-1)]
  transfers between devices with their start and end apart: 4 -> 0, of which waited for: 4 -> 0; matrix products, arithmetic and copies ran while one was open for 4% -> 0% of each run, Pallas kernels for 0% -> 0%
where the time goes in v1:
time: 23.8 us; the launch traced here: 23.6 us
  Pallas kernels  22.3 us (94%)
  local copies, waits for them, and re-layouts  1.29 us (5%)
    pallas_call x1, Pallas kernels, per_device(): pl.pallas_call(functools.partial(kernel, n, ng, cluster, size ** (-0.5)),...  22.3 us
    unnamed x1, local copies, waits for them, and re-layouts  1.29 us

profile of v1, /device:TPU:0, one launch (start us, length us, event | category | flops | bytes accessed | tf_op | source)
XLA Modules:
  0.0 23.6 jit_solution(13923268254882368705)
XLA Ops:
  0.0 22.3 %shard_map.55 = bf16[1,1280]{1,0:T(2,128)(2,1)} custom-call(bf16[16,128]{1,0:T(8,128)(2,1)} %bitcast.3, bf16[8,2,512,128]{3,2,1,0:T(8,128)(2,1)} %k_hbm.1, bf16[8,2,512,128]{3,2,1,0:T(8,128)(2,1)} %v_hbm.1, s32[8]{0:T(128)} %used.1, bf16[2048,5120]{1,0:T(8,128)(2,1)} %bitcast.2), custom_call_target="tpu_custom_call" | custom-call | tf_op jit(solution)/shard_map/pallas_call | solution.py:214
  22.3 1.3 %copy.7 = bf16[1,1280]{1,0:T(2,128)(2,1)} copy(bf16[1,1280]{1,0:T(2,128)(2,1)} %shard_map.55) | data formatting | bytes 5120

commit v2 on v1

--- a/solution.py
+++ b/solution.py
@@ -213,7 +213,7 @@
         f32, bf16 = jnp.float32, jnp.bfloat16
         return pl.pallas_call(
             functools.partial(kernel, n, ng, cluster, size ** (-0.5)),
-            out_shape=jax.ShapeDtypeStruct((1, width), bf16),
+            out_shape=pltpu.VMEM((1, width), bf16),
             in_specs=[anywhere, anywhere, anywhere, pl.BlockSpec(memory_space=pltpu.SMEM), anywhere],
             out_specs=pl.BlockSpec(memory_space=pltpu.VMEM),
             scratch_shapes=[

time: 23.8 us -> 22.5 us (0.945)
  local copies, waits for them, and re-layouts: 1.29 us -> 0.6 us
  Pallas kernels: 22.3 us -> 21.7 us
    unnamed x1, local copies, waits for them, and re-layouts: 1.29 us -> 0.6 us
    pallas_call x1, Pallas kernels: 22.3 us -> 21.7 us  [per_device(): pl.pallas_call(functools.partial(kernel, n, ng, cluster, size ** (-0.5)),...]
where the time goes in v2:
time: 22.5 us; the launch traced here: 22.3 us
  Pallas kernels  21.7 us (96%)
  local copies, waits for them, and re-layouts  0.6 us (3%)
    pallas_call x1, Pallas kernels, per_device(): pl.pallas_call(functools.partial(kernel, n, ng, cluster, size ** (-0.5)),...  21.7 us
    unnamed x1, local copies, waits for them, and re-layouts  0.6 us

profile of v2, /device:TPU:0, one launch (start us, length us, event | category | flops | bytes accessed | tf_op | source)
XLA Modules:
  0.0 22.3 jit_solution(15578654538968579574)
XLA Ops:
  0.0 21.7 %shard_map.55 = bf16[1,1280]{1,0:T(2,128)(2,1)S(1)} custom-call(bf16[16,128]{1,0:T(8,128)(2,1)} %bitcast.3, bf16[8,2,512,128]{3,2,1,0:T(8,128)(2,1)} %k_hbm.1, bf16[8,2,512,128]{3,2,1,0:T(8,128)(2,1)} %v_hbm.1, s32[8]{0:T(128)} %used.1, bf16[2048,5120]{1,0:T(8,128)(2,1)} %bitcast.2), custom_call_target="tpu_custom_call" | custom-call | tf_op jit(solution)/shard_map/pallas_call | solution.py:214
  21.7 0.6 %copy.7 = bf16[1,1280]{1,0:T(2,128)(2,1)} copy(bf16[1,1280]{1,0:T(2,128)(2,1)S(1)} %shard_map.55) | data formatting | bytes 5120

commit v3 on v0

v3 whole, which is shorter than its diff:
```python
import functools

import jax
import jax.numpy as jnp
from jax import lax
from jax.experimental import pallas as pl
from jax.experimental.pallas import tpu as pltpu
from jax.sharding import PartitionSpec as P

MESH = pl.DeviceIdType.MESH
CLUSTER = 2


def flip(index, bits):
    out, bit = index, 1
    while bit <= bits:
        if bits & bit:
            out = out + bit - 2 * bit * lax.rem(index // bit, 2)
        bit *= 2
    return out


def kernel(
    n, ng, cluster, scale,
    q_hbm, k_hbm, v_hbm, used, w_hbm, out_ref,
    q_all, k_v, v_v, w_v, made, parts, lhs, term, landed,
    q_sem, k_sem, v_sem, w_sem, q_send, q_recv, a_send, a_recv, t_send, t_recv,
):
    me, mg = lax.axis_index("seq"), lax.axis_index("group")
    batch, heads, stretch, size = k_v.shape
    rows = q_all.shape[1]
    per_head = rows // heads
    rf = rows // cluster
    f = lax.rem(me, cluster)
    width = out_ref.shape[1]
    depth = rf * size

    q_load = pltpu.make_async_copy(q_hbm, q_all.at[0], q_sem)
    q_load.start()
    barrier = pltpu.get_barrier_semaphore()
    partners = [(j, 0) for j in range(1, n)]
    partners += [(t, dg) for t in range(cluster) for dg in range(1, ng)]
    for j, dg in partners:
        pl.semaphore_signal(
            barrier, inc=1, device_id={"seq": flip(me, j), "group": flip(mg, dg)}, device_id_type=MESH
        )

    k_load = pltpu.make_async_copy(k_hbm, k_v, k_sem)
    v_load = pltpu.make_async_copy(v_hbm, v_v, v_sem)
    w_row = pl.multiple_of(f * depth, depth)
    w_loads = [
        pltpu.make_async_copy(
            w_hbm.at[pl.ds(w_row, depth), pl.ds(pl.multiple_of(flip(mg, dg) * width, width), width)],
            w_v.at[dg],
            w_sem.at[dg],
        )
        for dg in range(ng)
    ]
    for load in [k_load, v_load] + w_loads:
        load.start()
    lhs[...] = jnp.zeros_like(lhs)
    place = me * stretch + lax.broadcasted_iota(jnp.int32, (rows, stretch), 1)
    head_of = lax.broadcasted_iota(jnp.int32, (rows, size), 0) // per_head
    lane = lax.broadcasted_iota(jnp.int32, (rows, size), 1)

    def to_seq(src, dst, send, recv, j):
        return pltpu.make_async_remote_copy(
            src_ref=src, dst_ref=dst, send_sem=send.at[j], recv_sem=recv.at[j],
            device_id={"seq": flip(me, j), "group": mg}, device_id_type=MESH,
        )

    q_load.wait()
    pl.semaphore_wait(barrier, len(partners))
    q_out = [to_seq(q_all.at[0], q_all.at[j], q_send, q_recv, j) for j in range(1, n)]
    for copy in q_out[::-1]:
        copy.start()
    k_load.wait()
    v_load.wait()

    a_out = []
    for c in range(n // cluster):
        for i in range(cluster):
            j = c * cluster + i
            if j:
                q_out[j - 1].wait_recv()
        for i in range(cluster):
            j = c * cluster + i
            b = flip(me, j)
            q = q_all[j]
            split_q = jnp.concatenate(
                [jnp.where(head_of == h, q, jnp.zeros_like(q)) for h in range(heads)], axis=1
            )
            keys = jnp.concatenate([k_v[b, h] for h in range(heads)], axis=1)
            logit = lax.dot_general(
                split_q, keys, (((1,), (1,)), ((), ())), preferred_element_type=jnp.float32
            ) * scale
            filled = place < used[b]
            logit = jnp.where(filled, logit, -1e30)
            top = jnp.max(logit, axis=1, keepdims=True).astype(jnp.bfloat16).astype(jnp.float32)
            part = jnp.where(filled, jnp.exp(logit - top), 0.0)
            weight_sum = jnp.sum(part, axis=1, keepdims=True)
            high = part.astype(jnp.bfloat16)
            low = (part - high.astype(jnp.float32)).astype(jnp.bfloat16)
            values = jnp.concatenate([v_v[b, h] for h in range(heads)], axis=1)
            both = jnp.dot(
                jnp.concatenate([high, low], axis=0), values, preferred_element_type=jnp.float32
            )
            both = both[:rows] + both[rows:]
            read = jnp.concatenate(
                [
                    both[h * per_head : (h + 1) * per_head, h * size : (h + 1) * size]
                    for h in range(heads)
                ],
                axis=0,
            )
            read_high = read.astype(jnp.bfloat16).astype(jnp.float32)
            sum_high = weight_sum.astype(jnp.bfloat16).astype(jnp.float32)
            stat = jnp.where(lane == 0, top, jnp.where(lane == 1, sum_high, weight_sum - sum_high))
            for kind, tile in enumerate((read_high, read - read_high, stat)):
                for piece in range(cluster):
                    made[c, piece, kind, i * rf : (i + 1) * rf] = tile[
                        piece * rf : (piece + 1) * rf
                    ].astype(jnp.bfloat16)
        for i in range(cluster):
            j = c * cluster + i
            if j:
                copy = to_seq(made.at[c, flip(f, i)], parts.at[j], a_send, a_recv, j)
                copy.start()
                a_out.append(copy)

    def arranged(tile, p):
        tile = tile.astype(jnp.float32)
        return jnp.concatenate(
            [tile[(t ^ p) * rf : ((t ^ p) + 1) * rf] for t in range(cluster)], axis=0
        )

    got = [[arranged(made[0, f, kind], 0) for kind in range(3)]]
    for j in range(1, n):
        a_out[j - 1].wait_recv()
    for j in range(1, n):
        got.append([arranged(parts[j, kind], j % cluster) for kind in range(3)])
    best = functools.reduce(jnp.maximum, [stat[:, 0:1] for _, _, stat in got])
    weights = [jnp.exp(stat[:, 0:1] - best) for _, _, stat in got]
    total_weight = sum(w * (stat[:, 1:2] + stat[:, 2:3]) for w, (_, _, stat) in zip(weights, got))
    read = sum(w * (high + low) for w, (high, low, _) in zip(weights, got)) / total_weight
    for t in range(cluster):
        for r in range(rf):
            lhs[t : t + 1, r * size : (r + 1) * size] = read[t * rf + r : t * rf + r + 1]
    token = lhs[...].astype(jnp.bfloat16)

    for load in w_loads:
        load.wait()
    t_out = []
    for dg in reversed(range(ng)):
        out = jnp.dot(token, w_v[dg], preferred_element_type=jnp.float32)
        for t in range(cluster):
            if t == 0 and dg == 0:
                own = out[:1]
                continue
            slot = t * ng + dg
            term[slot] = out[t : t + 1]
            copy = pltpu.make_async_remote_copy(
                src_ref=term.at[slot], dst_ref=landed.at[slot],
                send_sem=t_send.at[slot], recv_sem=t_recv.at[slot],
                device_id={"seq": flip(me, t), "group": flip(mg, dg)}, device_id_type=MESH,
            )
            copy.start()
            t_out.append(copy)
    for copy in t_out:
        copy.wait_recv()
    for slot in range(1, cluster * ng):
        own += landed[slot]
    out_ref[...] = own.astype(out_ref.dtype)
    for copy in q_out + a_out + t_out:
        copy.wait_send()


def solution(mesh):
    n, ng = mesh.shape["seq"], mesh.shape["group"]

    def per_device(new_queries, stored_keys, stored_values, used_length, out_weight):
        batch, heads, stretch, size = stored_keys.shape
        group = new_queries.shape[2]
        rows = heads * group
        model = out_weight.shape[-1]
        cluster, width = CLUSTER, model // ng
        rf = rows // cluster
        dma = pltpu.SemaphoreType.DMA
        anywhere = pl.BlockSpec(memory_space=pl.ANY)
        f32, bf16 = jnp.float32, jnp.bfloat16
        return pl.pallas_call(
            functools.partial(kernel, n, ng, cluster, size ** (-0.5)),
            out_shape=pltpu.VMEM((1, width), bf16),
            in_specs=[anywhere, anywhere, anywhere, pl.BlockSpec(memory_space=pltpu.SMEM), anywhere],
            out_specs=pl.BlockSpec(memory_space=pltpu.VMEM),
            scratch_shapes=[
                pltpu.VMEM((n, rows, size), bf16),
                pltpu.VMEM(stored_keys.shape, bf16),
                pltpu.VMEM(stored_values.shape, bf16),
                pltpu.VMEM((ng, rf * size, width), bf16),
                pltpu.VMEM((n // cluster, cluster, 3, cluster * rf, size), bf16),
                pltpu.VMEM((n, 3, cluster * rf, size), bf16),
                pltpu.VMEM((8, rf * size), f32),
                pltpu.VMEM((cluster * ng, 1, width), f32),
                pltpu.VMEM((cluster * ng, 1, width), f32),
                dma, dma, dma, dma((ng,)),
                dma((n,)), dma((n,)), dma((n,)), dma((n,)),
                dma((cluster * ng,)), dma((cluster * ng,)),
            ],
            compiler_params=pltpu.CompilerParams(collective_id=0, has_side_effects=True),
        )(
            new_queries.reshape(rows, size),
            stored_keys,
            stored_values,
            used_length,
            out_weight.reshape(rows * size, model),
        )

    return jax.shard_map(
        per_device,
        mesh=mesh,
        in_specs=(
            P("seq", "group", None, None),
            P(None, "group", "seq", None),
            P(None, "group", "seq", None),
            P(),
            P("group", None, None, None),
        ),
        out_specs=P("seq", "group"),
        check_vma=False,
    )
```

time: 128 us -> 22.1 us (0.17)
  waiting for transfers between devices: 47.1 us -> 0 us
  blocking collectives: 32.5 us -> 0 us
  Pallas kernels: 0 us -> 21.2 us
  matrix products: 18 us -> 0 us
  between operations: 13.4 us -> 0.01 us
  starting transfers between devices: 12.1 us -> 0 us
  other arithmetic: 2.43 us -> 0 us
  local copies, waits for them, and re-layouts: 1.92 us -> 0.6 us
    all_gather x1 -> x0, blocking collectives: 32.5 us -> none  [per_device(): all_queries = lax.all_gather(new_queries, 'seq', axis=0, tiled=True)]
    unnamed x2 -> x0, waiting for transfers between devices: 32.1 us -> none
    pallas_call x0 -> x1, Pallas kernels: none -> 21.2 us  [per_device(): pl.pallas_call(functools.partial(kernel, n, ng, cluster, size ** (-0.5)),...]
    dot_general x3 -> x0, matrix products: 18 us -> none  [the longest x1 13.4 us: per_device(): jnp.einsum('bkgd,kgdm->bm', read, out_weight, preferred_element_type=jnp....]
    all_to_all x3 -> x0, waiting for transfers between devices: 15.1 us -> none  [the longest x1 6.74 us: per_device(): lax.all_to_all(read_sum[None], 'seq', split_axis=1, concat_axis=0, tiled=...]
    all_to_all x3 -> x0, starting transfers between devices: 12.1 us -> none  [the longest x1 5.46 us: per_device(): lax.all_to_all(top[None], 'seq', split_axis=1, concat_axis=0, tiled=True)]
    reduce_sum x3 -> x0, other arithmetic: 1.59 us -> none  [the longest x1 1.49 us: per_device(): weight_sum = jnp.sum(part, axis=-1)]
    unnamed x3 -> x1, local copies, waits for them, and re-layouts: 1.92 us -> 0.6 us
  transfers between devices with their start and end apart: 4 -> 0, of which waited for: 4 -> 0; matrix products, arithmetic and copies ran while one was open for 4% -> 0% of each run, Pallas kernels for 0% -> 0%
where the time goes in v3:
time: 22.1 us; the launch traced here: 21.9 us
  Pallas kernels  21.2 us (96%)
  local copies, waits for them, and re-layouts  0.6 us (3%)
    pallas_call x1, Pallas kernels, per_device(): pl.pallas_call(functools.partial(kernel, n, ng, cluster, size ** (-0.5)),...  21.2 us
    unnamed x1, local copies, waits for them, and re-layouts  0.6 us

profile of v3, /device:TPU:0, one launch (start us, length us, event | category | flops | bytes accessed | tf_op | source)
XLA Modules:
  0.0 21.9 jit_solution(7454908191153191595)
XLA Ops:
  0.0 21.2 %shard_map.55 = bf16[1,1280]{1,0:T(2,128)(2,1)S(1)} custom-call(bf16[16,128]{1,0:T(8,128)(2,1)} %bitcast.3, bf16[8,2,512,128]{3,2,1,0:T(8,128)(2,1)} %k_hbm.1, bf16[8,2,512,128]{3,2,1,0:T(8,128)(2,1)} %v_hbm.1, s32[8]{0:T(128)} %used.1, bf16[2048,5120]{1,0:T(8,128)(2,1)} %bitcast.2), custom_call_target="tpu_custom_call" | custom-call | tf_op jit(solution)/shard_map/pallas_call | solution.py:191
  21.3 0.6 %copy.7 = bf16[1,1280]{1,0:T(2,128)(2,1)} copy(bf16[1,1280]{1,0:T(2,128)(2,1)S(1)} %shard_map.55) | data formatting | bytes 5120

commit v4 on v3

--- a/solution.py
+++ b/solution.py
@@ -9,6 +9,7 @@
 
 MESH = pl.DeviceIdType.MESH
 CLUSTER = 2
+CHUNK = 1
 
 
 def flip(index, bits):
@@ -23,8 +24,8 @@
 def kernel(
     n, ng, cluster, scale,
     q_hbm, k_hbm, v_hbm, used, w_hbm, out_ref,
-    q_all, k_v, v_v, w_v, made, parts, lhs, term, landed,
-    q_sem, k_sem, v_sem, w_sem, q_send, q_recv, a_send, a_recv, t_send, t_recv,
+    q_all, k_v, v_v, w_v, made, parts, stat_made, stats, lhs, term, landed,
+    q_sem, k_sem, v_sem, w_sem, q_send, q_recv, s_send, s_recv, a_send, a_recv, t_send, t_recv,
 ):
     me, mg = lax.axis_index("seq"), lax.axis_index("group")
     batch, heads, stretch, size = k_v.shape
@@ -40,7 +41,7 @@
     barrier = pltpu.get_barrier_semaphore()
     partners = [(j, 0) for j in range(1, n)]
     partners += [(t, dg) for t in range(cluster) for dg in range(1, ng)]
-    for j, dg in partners:
+    for j, dg in reversed(partners):
         pl.semaphore_signal(
             barrier, inc=1, device_id={"seq": flip(me, j), "group": flip(mg, dg)}, device_id_type=MESH
         )
@@ -62,6 +63,7 @@
     place = me * stretch + lax.broadcasted_iota(jnp.int32, (rows, stretch), 1)
     head_of = lax.broadcasted_iota(jnp.int32, (rows, size), 0) // per_head
     lane = lax.broadcasted_iota(jnp.int32, (rows, size), 1)
+    line, half = lax.broadcasted_iota(jnp.int32, (rows, size), 0), size // 2
 
     def to_seq(src, dst, send, recv, j):
         return pltpu.make_async_remote_copy(
@@ -77,14 +79,16 @@
     k_load.wait()
     v_load.wait()
 
-    a_out = []
-    for c in range(n // cluster):
-        for i in range(cluster):
-            j = c * cluster + i
+    a_out, s_out = [], []
+    clusters = n // cluster
+    for start in range(0, clusters, CHUNK):
+        chunk = range(start, min(start + CHUNK, clusters))
+        members = [c * cluster + i for c in chunk for i in range(cluster)]
+        for j in members:
             if j:
                 q_out[j - 1].wait_recv()
-        for i in range(cluster):
-            j = c * cluster + i
+        logits, parts_of, tops, sums, reads = {}, {}, {}, {}, {}
+        for j in members:
             b = flip(me, j)
             q = q_all[j]
             split_q = jnp.concatenate(
@@ -94,55 +98,75 @@
             logit = lax.dot_general(
                 split_q, keys, (((1,), (1,)), ((), ())), preferred_element_type=jnp.float32
             ) * scale
-            filled = place < used[b]
-            logit = jnp.where(filled, logit, -1e30)
-            top = jnp.max(logit, axis=1, keepdims=True).astype(jnp.bfloat16).astype(jnp.float32)
-            part = jnp.where(filled, jnp.exp(logit - top), 0.0)
-            weight_sum = jnp.sum(part, axis=1, keepdims=True)
+            logits[j] = jnp.where(place < used[b], logit, -1e30)
+        for j in members:
+            tops[j] = jnp.max(logits[j], axis=1, keepdims=True)
+        for j in members:
+            filled = place < used[flip(me, j)]
+            part = jnp.where(filled, jnp.exp(logits[j] - tops[j]), 0.0)
             high = part.astype(jnp.bfloat16)
             low = (part - high.astype(jnp.float32)).astype(jnp.bfloat16)
+            parts_of[j] = jnp.concatenate([high, low], axis=0)
+            sums[j] = jnp.sum(part, axis=1, keepdims=True)
+        for j in members:
+            b = flip(me, j)
             values = jnp.concatenate([v_v[b, h] for h in range(heads)], axis=1)
-            both = jnp.dot(
-                jnp.concatenate([high, low], axis=0), values, preferred_element_type=jnp.float32
-            )
+            both = jnp.dot(parts_of[j], values, preferred_element_type=jnp.float32)
             both = both[:rows] + both[rows:]
-            read = jnp.concatenate(
+            reads[j] = jnp.concatenate(
                 [
                     both[h * per_head : (h + 1) * per_head, h * size : (h + 1) * size]
                     for h in range(heads)
                 ],
                 axis=0,
             )
-            read_high = read.astype(jnp.bfloat16).astype(jnp.float32)
-            sum_high = weight_sum.astype(jnp.bfloat16).astype(jnp.float32)
-            stat = jnp.where(lane == 0, top, jnp.where(lane == 1, sum_high, weight_sum - sum_high))
-            for kind, tile in enumerate((read_high, read - read_high, stat)):
+        for c in reversed(chunk):
+            for piece in range(cluster):
+                cut = slice(piece * rf, (piece + 1) * rf)
+                pick = [c * cluster + i for i in range(cluster)]
+                top = jnp.concatenate([tops[j][cut] for j in pick], axis=0)
+                weight_sum = jnp.concatenate([sums[j][cut] for j in pick], axis=0)
+                spread = jnp.where(lane == line, top, jnp.where(lane == line + half, weight_sum, 0.0))
+                stat_made[c, piece] = jnp.sum(spread, axis=0, keepdims=True)
+            for i in reversed(range(cluster)):
+                j = c * cluster + i
+                if j:
+                    s_out.append(to_seq(stat_made.at[c, flip(f, i)], stats.at[j], s_send, s_recv, j))
+                    s_out[-1].start()
+            for i in range(cluster):
                 for piece in range(cluster):
-                    made[c, piece, kind, i * rf : (i + 1) * rf] = tile[
+                    made[c, piece, i * rf : (i + 1) * rf] = reads[c * cluster + i][
                         piece * rf : (piece + 1) * rf
-                    ].astype(jnp.bfloat16)
-        for i in range(cluster):
-            j = c * cluster + i
-            if j:
-                copy = to_seq(made.at[c, flip(f, i)], parts.at[j], a_send, a_recv, j)
-                copy.start()
-                a_out.append(copy)
+                    ]
+            for i in reversed(range(cluster)):
+                j = c * cluster + i
+                if j:
+                    a_out.append(to_seq(made.at[c, flip(f, i)], parts.at[j], a_send, a_recv, j))
+                    a_out[-1].start()
 
     def arranged(tile, p):
-        tile = tile.astype(jnp.float32)
         return jnp.concatenate(
             [tile[(t ^ p) * rf : ((t ^ p) + 1) * rf] for t in range(cluster)], axis=0
         )
 
-    got = [[arranged(made[0, f, kind], 0) for kind in range(3)]]
+    for copy in s_out:
+        copy.wait_recv()
+    tops, sums = [], []
+    for j in range(n):
+        row = jnp.broadcast_to(stats[j] if j else stat_made[0, f], (rows, size))
+        tops.append(arranged(jnp.sum(jnp.where(lane == line, row, 0.0), axis=1, keepdims=True), j % cluster))
+        sums.append(
+            arranged(jnp.sum(jnp.where(lane == line + half, row, 0.0), axis=1, keepdims=True), j % cluster)
+        )
+    best = functools.reduce(jnp.maximum, tops)
+    weights = [jnp.exp(top - best) for top in tops]
+    total_weight = sum(w * weight_sum for w, weight_sum in zip(weights, sums))
+    weights = [w / total_weight for w in weights]
+    for copy in a_out:
+        copy.wait_recv()
+    read = weights[0] * made[0, f]
     for j in range(1, n):
-        a_out[j - 1].wait_recv()
-    for j in range(1, n):
-        got.append([arranged(parts[j, kind], j % cluster) for kind in range(3)])
-    best = functools.reduce(jnp.maximum, [stat[:, 0:1] for _, _, stat in got])
-    weights = [jnp.exp(stat[:, 0:1] - best) for _, _, stat in got]
-    total_weight = sum(w * (stat[:, 1:2] + stat[:, 2:3]) for w, (_, _, stat) in zip(weights, got))
-    read = sum(w * (high + low) for w, (high, low, _) in zip(weights, got)) / total_weight
+        read += weights[j] * arranged(parts[j], j % cluster)
     for t in range(cluster):
         for r in range(rf):
             lhs[t : t + 1, r * size : (r + 1) * size] = read[t * rf + r : t * rf + r + 1]
@@ -171,7 +195,7 @@
     for slot in range(1, cluster * ng):
         own += landed[slot]
     out_ref[...] = own.astype(out_ref.dtype)
-    for copy in q_out + a_out + t_out:
+    for copy in q_out + s_out + a_out + t_out:
         copy.wait_send()
 
 
@@ -198,13 +222,15 @@
                 pltpu.VMEM(stored_keys.shape, bf16),
                 pltpu.VMEM(stored_values.shape, bf16),
                 pltpu.VMEM((ng, rf * size, width), bf16),
-                pltpu.VMEM((n // cluster, cluster, 3, cluster * rf, size), bf16),
-                pltpu.VMEM((n, 3, cluster * rf, size), bf16),
+                pltpu.VMEM((n // cluster, cluster, rows, size), f32),
+                pltpu.VMEM((n, rows, size), f32),
+                pltpu.VMEM((n // cluster, cluster, 1, size), f32),
+                pltpu.VMEM((n, 1, size), f32),
                 pltpu.VMEM((8, rf * size), f32),
                 pltpu.VMEM((cluster * ng, 1, width), f32),
                 pltpu.VMEM((cluster * ng, 1, width), f32),
                 dma, dma, dma, dma((ng,)),
-                dma((n,)), dma((n,)), dma((n,)), dma((n,)),
+                dma((n,)), dma((n,)), dma((n,)), dma((n,)), dma((n,)), dma((n,)),
                 dma((cluster * ng,)), dma((cluster * ng,)),
             ],
             compiler_params=pltpu.CompilerParams(collective_id=0, has_side_effects=True),

time: 22.1 us -> 21.2 us (0.959)
  Pallas kernels: 21.2 us -> 20.4 us
    pallas_call x1, Pallas kernels: 21.2 us -> 20.4 us  [per_device(): pl.pallas_call(functools.partial(kernel, n, ng, cluster, size ** (-0.5)),...]
where the time goes in v4:
time: 21.2 us; the launch traced here: 21 us
  Pallas kernels  20.4 us (96%)
  local copies, waits for them, and re-layouts  0.6 us (3%)
    pallas_call x1, Pallas kernels, per_device(): pl.pallas_call(functools.partial(kernel, n, ng, cluster, size ** (-0.5)),...  20.4 us
    unnamed x1, local copies, waits for them, and re-layouts  0.6 us

profile of v4, /device:TPU:0, one launch (start us, length us, event | category | flops | bytes accessed | tf_op | source)
XLA Modules:
  0.0 21.0 jit_solution(3736835481384840309)
XLA Ops:
  0.0 20.4 %shard_map.55 = bf16[1,1280]{1,0:T(2,128)(2,1)S(1)} custom-call(bf16[16,128]{1,0:T(8,128)(2,1)} %bitcast.3, bf16[8,2,512,128]{3,2,1,0:T(8,128)(2,1)} %k_hbm.1, bf16[8,2,512,128]{3,2,1,0:T(8,128)(2,1)} %v_hbm.1, s32[8]{0:T(128)} %used.1, bf16[2048,5120]{1,0:T(8,128)(2,1)} %bitcast.2), custom_call_target="tpu_custom_call" | custom-call | tf_op jit(solution)/shard_map/pallas_call | solution.py:215
  20.4 0.6 %copy.7 = bf16[1,1280]{1,0:T(2,128)(2,1)} copy(bf16[1,1280]{1,0:T(2,128)(2,1)S(1)} %shard_map.55) | data formatting | bytes 5120

commit v5 on v4

--- a/solution.py
+++ b/solution.py
@@ -175,7 +175,7 @@
     for load in w_loads:
         load.wait()
     t_out = []
-    for dg in reversed(range(ng)):
+    for dg in [*range(ng // 2, ng), *range(ng // 2)]:
         out = jnp.dot(token, w_v[dg], preferred_element_type=jnp.float32)
         for t in range(cluster):
             if t == 0 and dg == 0:

time: 21.2 us -> 20.7 us (0.976)
  Pallas kernels: 20.4 us -> 19.9 us
    pallas_call x1, Pallas kernels: 20.4 us -> 19.9 us  [per_device(): pl.pallas_call(functools.partial(kernel, n, ng, cluster, size ** (-0.5)),...]
where the time goes in v5:
time: 20.7 us; the launch traced here: 20.5 us
  Pallas kernels  19.9 us (96%)
  local copies, waits for them, and re-layouts  0.6 us (3%)
    pallas_call x1, Pallas kernels, per_device(): pl.pallas_call(functools.partial(kernel, n, ng, cluster, size ** (-0.5)),...  19.9 us
    unnamed x1, local copies, waits for them, and re-layouts  0.6 us

profile of v5, /device:TPU:0, one launch (start us, length us, event | category | flops | bytes accessed | tf_op | source)
XLA Modules:
  0.0 20.5 jit_solution(7242987993684538279)
XLA Ops:
  0.0 19.9 %shard_map.55 = bf16[1,1280]{1,0:T(2,128)(2,1)S(1)} custom-call(bf16[16,128]{1,0:T(8,128)(2,1)} %bitcast.3, bf16[8,2,512,128]{3,2,1,0:T(8,128)(2,1)} %k_hbm.1, bf16[8,2,512,128]{3,2,1,0:T(8,128)(2,1)} %v_hbm.1, s32[8]{0:T(128)} %used.1, bf16[2048,5120]{1,0:T(8,128)(2,1)} %bitcast.2), custom_call_target="tpu_custom_call" | custom-call | tf_op jit(solution)/shard_map/pallas_call | solution.py:215
  19.9 0.6 %copy.7 = bf16[1,1280]{1,0:T(2,128)(2,1)} copy(bf16[1,1280]{1,0:T(2,128)(2,1)S(1)} %shard_map.55) | data formatting | bytes 5120
